TPU v7x, 32 devices: a whole 2x2x4 slice. The times are simulated.
32 devices in a mesh: gx: 4 (over y, x), gy: 2 (over core), gz: 4 (over z).
Axes of the slice: x: 2, y: 2, z: 4, core: 2. Of those that a mesh axis runs over, the one named last changes fastest.
Arguments:
- pair: bfloat16 [128, 1024, 1024], P('gz', 'gy', 'gx'), may hold values from -6 to 6
- pair_mask: int32 [1024, 1024], P('gy', 'gx'), may hold values 0 or 1
- in_gain: float32 [128], replicated, may hold values from 0.5 to 2
- w_left: bfloat16 [128, 128], P(None, 'gz'), may hold values from -0.5 to 0.5
- w_left_gate: bfloat16 [128, 128], P(None, 'gz'), may hold values from -0.5 to 0.5
- w_right: bfloat16 [128, 128], P(None, 'gz'), may hold values from -0.5 to 0.5
- w_right_gate: bfloat16 [128, 128], P(None, 'gz'), may hold values from -0.5 to 0.5
- w_out_gate: bfloat16 [128, 128], P(None, 'gz'), may hold values from -0.5 to 0.5
- out_gain: float32 [128], P('gz'), may hold values from 0.5 to 2
- w_out: bfloat16 [128, 128], P(None, 'gz'), may hold values from -0.5 to 0.5
Outputs:
- update: bfloat16 [128, 1024, 1024], P('gz', 'gy', 'gx')
All inputs are finite; a program needn't handle non-finite values. No bound on the sum of `pair_mask` on one device may be relied on, other than what follows from the above.
Results may differ from a plain program's by a relative error of at most 0.0078.
Values may be sent and summed in bfloat16 or wider, within the bound.
A program may use at most 192 MiB of HBM per device.

v0:
```python
import jax
import jax.numpy as jnp
from jax import lax
from jax.sharding import PartitionSpec as P

epsilon = 1e-05


def local(
    pair,
    pair_mask,
    in_gain,
    w_left,
    w_left_gate,
    w_right,
    w_right_gate,
    w_out_gate,
    out_gain,
    w_out,
):
    gathered = lax.all_gather(pair, "gz", axis=0, tiled=True).astype(jnp.float32)
    average = jnp.mean(gathered, axis=0)
    centered = gathered - average
    spread = jnp.mean(jnp.square(centered), axis=0)
    normed = (centered * lax.rsqrt(spread + epsilon) * in_gain[:, None, None]).astype(jnp.bfloat16)
    mask_float = pair_mask.astype(jnp.float32)[None]

    def project(weight):
        return jnp.einsum("cik,ch->hik", normed, weight, preferred_element_type=jnp.float32)

    left_rows = (mask_float * jax.nn.sigmoid(project(w_left_gate)) * project(w_left)).astype(
        jnp.bfloat16
    )
    right_rows = (mask_float * jax.nn.sigmoid(project(w_right_gate)) * project(w_right)).astype(
        jnp.bfloat16
    )
    out_gate = jax.nn.sigmoid(
        jnp.einsum("cij,cd->dij", normed, w_out_gate, preferred_element_type=jnp.float32)
    )
    left_group, right_group = (
        lax.all_to_all(left_rows, "gx", split_axis=0, concat_axis=2, tiled=True),
        lax.all_to_all(right_rows, "gx", split_axis=0, concat_axis=2, tiled=True),
    )
    full_product = lax.dot_general(
        left_group,
        lax.all_gather(right_group, "gy", axis=1, tiled=True),
        (((2,), (2,)), ((0,), (0,))),
        preferred_element_type=jnp.float32,
    )
    mixed_sum = lax.all_to_all(full_product, "gx", split_axis=2, concat_axis=0, tiled=True)
    channel_count = lax.axis_size("gz") * mixed_sum.shape[0]
    sum_terms = lax.psum(jnp.sum(mixed_sum, axis=0), "gz")
    mix_average = sum_terms / channel_count
    mix_centered = mixed_sum - mix_average
    mix_spread = lax.psum(jnp.sum(jnp.square(mix_centered), axis=0), "gz") / channel_count
    local_mix = (mix_centered * lax.rsqrt(mix_spread + epsilon) * out_gain[:, None, None]).astype(
        jnp.bfloat16
    )
    normed_mix = lax.all_gather(local_mix, "gz", axis=0, tiled=True)
    projected = jnp.einsum("hij,hd->dij", normed_mix, w_out, preferred_element_type=jnp.float32)
    return (out_gate * projected).astype(jnp.bfloat16)


def solution(mesh):
    placed = (
        P("gz", "gy", "gx"),
        P("gy", "gx"),
        P(),
        P(None, "gz"),
        P(None, "gz"),
        P(None, "gz"),
        P(None, "gz"),
        P(None, "gz"),
        P("gz"),
        P(None, "gz"),
    )
    return jax.shard_map(
        local, mesh=mesh, in_specs=placed, out_specs=P("gz", "gy", "gx"), check_vma=False
    )
```

profile of v0, /device:TPU:8, one launch (start us, length us, event | category | flops | bytes accessed | tf_op | source)
XLA Modules:
  0.0 1979.6 jit_solution(8913950968688597543)
XLA Ops:
  6.5 0.0 copy-start
  6.5 0.0 all-gather.4.cloned.1.call-start
  6.5 0.7 all-gather.4.cloned.1.call-update
  7.3 0.0 all-gather.6.cloned.1.call-start
  7.3 1.1 convert_element_type.23
  8.4 560.1 %all-gather.4.cloned.1.call-done = bf16[128,512,256]{2,1,0:T(8,128)(2,1)} async-done(((bf16[32,512,256]{2,1,0:T(8,128)(2,1)}), bf16[128,512,256]{2,1,0:T(8,128)(2,1)}) %all-gather.4.cloned.1.call-update) | async-done | bytes 33554448 | tf_op jit(solution)/shard_map/all_gather | solution.py:21
  568.5 11.4 convert_reduce_fusion
  580.0 0.0 copy-start.4
  580.0 11.7 fusion.2
  591.6 0.1 add_rsqrt_fusion.1
  591.7 0.0 copy-done.4
  591.7 23.0 %fusion.4 = bf16[128,512,256]{2,1,0:T(8,128)(2,1)} fusion(bf16[128,512,256]{2,1,0:T(8,128)(2,1)} %all-gather.4.cloned.1.call-done, f32[128]{0:T(128)S(1)} %copy-done.4, f32[512,256]{1,0:T(8,128)S(1)} %add_rsqrt_fusion.1, f32[512,256]{1,0:T(8,128)S(1)} %broadcast_multiply_fusion.1), kind=kLoop, calls=%fused_computation.6 | loop fusion | flops 83886080 | bytes 68157952 | tf_op jit(solution)/shard_map/convert_element_type | solution.py:25
  614.8 0.0 copy-done
  614.8 0.0 copy-start.6
  614.8 35.7 %fusion.11 = f32[512,256,32]{1,2,0:T(8,128)} fusion(bf16[128,512,256]{2,1,0:T(8,128)(2,1)} %fusion.4, bf16[128,32]{0,1:T(8,128)(2,1)S(1)} %copy-done), kind=kOutput, calls=%fused_computation.13 | convolution fusion | flops 1073741824 | bytes 50339840 | tf_op jit(solution)/shard_map/cik,ch->hik/dot_general | solution.py:29
  650.5 0.0 copy-done.6
  650.5 38.1 %fusion.28 = bf16[32,512,256]{2,0,1:T(8,128)(2,1)} fusion(bf16[128,512,256]{2,1,0:T(8,128)(2,1)} %fusion.4, f32[512,256,32]{1,2,0:T(8,128)} %fusion.11, f32[512,256]{1,0:T(8,128)S(1)} %convert_element_type.23, bf16[128,32]{0,1:T(8,128)(2,1)S(1)} %copy-done.6), kind=kOutput, calls=%fused_computation.32 | convolution fusion | flops 1098907648 | bytes 59252736 | tf_op jit(solution)/shard_map/cik,ch->hik/dot_general | solution.py:29
  688.6 11.4 copy.27
  700.0 97.2 %all_to_all.54 = bf16[32,512,256]{2,1,0:T(8,128)(2,1)S(1)} all-to-all(bf16[32,512,256]{2,1,0:T(8,128)(2,1)} %copy.27), channel_id=1, replica_groups=mesh['gx'=4,'gy'=2,'gz'=4] {'gx'}, dimensions={0} | all-to-all | bytes 16777216 | tf_op jit(solution)/shard_map/all_to_all | solution.py:42
  797.2 7.3 copy.52
  804.5 0.0 copy-start.2
  804.5 14.3 all_to_all.46
  818.8 0.0 all-gather.6.cloned.1.call-update
  818.8 0.0 copy-start.7
  818.8 0.0 all-reduce.3.cloned.1.call-start
  818.9 0.0 copy-done.2
  818.9 35.9 %fusion.7 = f32[512,256,32]{1,2,0:T(8,128)} fusion(bf16[128,512,256]{2,1,0:T(8,128)(2,1)} %fusion.4, bf16[128,32]{0,1:T(8,128)(2,1)S(1)} %copy-done.2), kind=kOutput, calls=%fused_computation.9 | convolution fusion | flops 1073741824 | bytes 50339840 | tf_op jit(solution)/shard_map/cik,ch->hik/dot_general | solution.py:29
  854.8 0.0 copy-done.7
  854.8 38.1 %fusion.25 = bf16[32,512,256]{2,0,1:T(8,128)(2,1)} fusion(bf16[128,512,256]{2,1,0:T(8,128)(2,1)} %fusion.4, f32[512,256,32]{1,2,0:T(8,128)} %fusion.7, f32[512,256]{1,0:T(8,128)S(1)} %convert_element_type.23, bf16[128,32]{0,1:T(8,128)(2,1)S(1)} %copy-done.7), kind=kOutput, calls=%fused_computation.31 | convolution fusion | flops 1098907648 | bytes 59252736 | tf_op jit(solution)/shard_map/cik,ch->hik/dot_general | solution.py:29
  892.9 11.4 copy.23
  904.2 95.8 %all_to_all.55 = bf16[32,512,256]{2,1,0:T(8,128)(2,1)S(1)} all-to-all(bf16[32,512,256]{2,1,0:T(8,128)(2,1)} %copy.23), channel_id=1, replica_groups=mesh['gx'=4,'gy'=2,'gz'=4] {'gx'}, dimensions={0} | all-to-all | bytes 16777216 | tf_op jit(solution)/shard_map/all_to_all | solution.py:41
  1000.0 7.3 copy.53
  1007.3 14.3 all_to_all.42
  1021.6 0.0 all-gather.6.cloned.1.call-done
  1021.6 17.0 fusion.37
  1038.6 17.6 copy.29
  1056.2 191.4 %all_to_all.56 = f32[8,512,1024]{1,0,2:T(8,128)} all-to-all(f32[8,512,1024]{1,0,2:T(8,128)} %copy.29), channel_id=1, replica_groups=mesh['gx'=4,'gy'=2,'gz'=4] {'gx'}, dimensions={2} | all-to-all | bytes 33554432 | tf_op jit(solution)/shard_map/all_to_all | solution.py:50
  1247.6 20.2 %copy.30 = f32[8,512,4,256]{3,0,2,1:T(8,128)} copy(f32[8,512,4,256]{1,0,3,2:T(8,128)} %bitcast.52) | data formatting | bytes 33554432 | tf_op jit(solution)/shard_map/all_to_all | solution.py:50
  1267.9 0.0 copy-start.5
  1267.9 9.5 bitcast_reduce_fusion
  1277.4 0.0 all-reduce.3.cloned.1.call-update
  1277.4 0.0 all-reduce.5.cloned.1.call-start
  1277.4 39.3 %all-reduce.3.cloned.1.call-done = f32[512,256]{1,0:T(8,128)} async-done(((f32[512,256]{1,0:T(8,128)}), f32[512,256]{1,0:T(8,128)}) %all-reduce.3.cloned.1.call-update) | async-done | bytes 524304 | tf_op jit(solution)/shard_map/psum | solution.py:52
  1316.7 1.1 broadcast_multiply_fusion
  1317.8 12.2 fusion.19
  1330.0 0.0 all-reduce.5.cloned.1.call-update
  1330.0 0.0 all-gather.8.cloned.1.call-start
  1330.1 38.6 %all-reduce.5.cloned.1.call-done = f32[512,256]{1,0:T(8,128)} async-done(((f32[512,256]{1,0:T(8,128)}), f32[512,256]{1,0:T(8,128)}) %all-reduce.5.cloned.1.call-update) | async-done | bytes 524304 | tf_op jit(solution)/shard_map/psum | solution.py:55
  1368.6 1.1 add_rsqrt_fusion
  1369.8 0.0 copy-done.5
  1369.8 0.0 copy-start.3
  1369.8 11.1 fusion.17
  1380.9 0.0 all-gather.8.cloned.1.call-update
  1380.9 0.0 copy-done.3
  1380.9 0.0 copy-start.8
  1380.9 35.8 %fusion.5 = f32[512,256,32]{1,2,0:T(8,128)} fusion(bf16[128,512,256]{2,1,0:T(8,128)(2,1)} %fusion.4, bf16[128,32]{0,1:T(8,128)(2,1)S(1)} %copy-done.3), kind=kOutput, calls=%fused_computation.7 | convolution fusion | flops 1073741824 | bytes 50339840 | tf_op jit(solution)/shard_map/cij,cd->dij/dot_general | solution.py:38
  1416.7 522.5 %all-gather.8.cloned.1.call-done = bf16[128,512,256]{2,0,1:T(8,128)(2,1)} async-done(((bf16[32,512,256]{2,0,1:T(8,128)(2,1)}), bf16[128,512,256]{2,0,1:T(8,128)(2,1)}) %all-gather.8.cloned.1.call-update) | async-done | bytes 33554448 | tf_op jit(solution)/shard_map/all_gather | solution.py:59
  1939.2 0.0 copy-done.8
  1939.2 0.0 copy-start.1
  1939.2 21.8 %fusion.24 = bf16[32,512,256]{2,0,1:T(8,128)(2,1)} fusion(bf16[128,512,256]{2,0,1:T(8,128)(2,1)} %all-gather.8.cloned.1.call-done, f32[512,256,32]{1,2,0:T(8,128)} %fusion.5, bf16[128,32]{0,1:T(8,128)(2,1)S(1)} %copy-done.8), kind=kOutput, calls=%fused_computation.30 | convolution fusion | flops 1094713344 | bytes 58728448 | tf_op jit(solution)/shard_map/hij,hd->dij/dot_general | solution.py:60
  1961.0 11.5 copy.31
  1972.6 0.0 copy-done.1
  (1 shorter events, 0.0 us)
Async XLA Ops:
  6.5 608.2 %copy-start = (bf16[128,32]{0,1:T(8,128)(2,1)S(1)}, bf16[128,32]{0,1:T(8,128)(2,1)}, u32[]{:S(2)}) copy-start(bf16[128,32]{0,1:T(8,128)(2,1)} %param.16) | copy-start | bytes 24580
  6.5 562.0 %all-gather.4.cloned.1.call-start = ((), (), s32[]{:S(2)}) async-start(), calls=%async_computation.3 | async-start | bytes 41943040 | tf_op jit(solution)/shard_map/all_gather | solution.py:21
  7.3 1014.4 %all-gather.6.cloned.1.call-start = ((), (), s32[]{:S(2)}) async-start(), calls=%async_computation.4 | async-start | bytes 25165824 | tf_op jit(solution)/shard_map/all_gather | solution.py:46
  580.0 11.8 copy-start.4
  614.8 35.7 %copy-start.6 = (bf16[128,32]{0,1:T(8,128)(2,1)S(1)}, bf16[128,32]{0,1:T(8,128)(2,1)}, u32[]{:S(2)}) copy-start(bf16[128,32]{0,1:T(8,128)(2,1)} %param.15) | copy-start | bytes 24580
  804.5 14.4 copy-start.2
  818.8 35.9 %copy-start.7 = (bf16[128,32]{0,1:T(8,128)(2,1)S(1)}, bf16[128,32]{0,1:T(8,128)(2,1)}, u32[]{:S(2)}) copy-start(bf16[128,32]{0,1:T(8,128)(2,1)} %param.13) | copy-start | bytes 24580
  818.8 497.9 %all-reduce.3.cloned.1.call-start = ((), (), s32[]{:S(2)}) async-start(), calls=%async_computation.5 | async-start | bytes 1048576 | tf_op jit(solution)/shard_map/psum | solution.py:52
  1267.9 101.9 %copy-start.5 = (f32[32]{0:T(128)S(1)}, f32[32]{0:T(128)}, u32[]{:S(2)}) copy-start(f32[32]{0:T(128)} %param.18) | copy-start | bytes 388
  1277.4 91.3 %all-reduce.5.cloned.1.call-start = ((), (), s32[]{:S(2)}) async-start(), calls=%async_computation.6 | async-start | bytes 1048576 | tf_op jit(solution)/shard_map/psum | solution.py:55
  1330.0 609.2 %all-gather.8.cloned.1.call-start = ((), (), s32[]{:S(2)}) async-start(), calls=%async_computation.7 | async-start | bytes 41943040 | tf_op jit(solution)/shard_map/all_gather | solution.py:59
  1369.8 11.1 copy-start.3
  1380.9 558.3 %copy-start.8 = (bf16[128,32]{0,1:T(8,128)(2,1)S(1)}, bf16[128,32]{0,1:T(8,128)(2,1)}, u32[]{:S(2)}) copy-start(bf16[128,32]{0,1:T(8,128)(2,1)} %param.19) | copy-start | bytes 24580
  1939.2 33.4 %copy-start.1 = (bf16[128,32]{0,1:T(8,128)(2,1)S(1)}, bf16[128,32]{0,1:T(8,128)(2,1)}, u32[]{:S(2)}) copy-start(bf16[128,32]{0,1:T(8,128)(2,1)} %param.16) | copy-start | bytes 24580
Sparse Core Ops, SparseCore 0:
  8.9 559.5 all-gather.3
  818.9 30.1 all-gather.5
  1277.5 39.1 all-reduce.2
  1330.1 38.4 all-reduce.4
  1381.0 558.1 all-gather.7
where the time goes:
time: 1990 us; the launch traced here: 1980 us
  waiting for transfers between devices  1160 us (58%)
  blocking collectives  384 us (19%)
  matrix products  222 us (11%)
  local copies, waits for them, and re-layouts  115 us (6%)
  other arithmetic  82.3 us (4%)
    all_gather x1, waiting for transfers between devices, local(): lax.all_gather(pair, 'gz', axis=0, tiled=True).astype(jnp.float32)  560 us
    all_gather x1, waiting for transfers between devices, local(): normed_mix = lax.all_gather(local_mix, 'gz', axis=0, tiled=True)  522 us
    all_to_all x1, blocking collectives, local(): lax.all_to_all(full_product, 'gx', split_axis=2, concat_axis=0, tiled=True)  191 us
    dot_general x4, matrix products, project(): jnp.einsum('cik,ch->hik', normed, weight, preferred_element_type=jnp.floa...  148 us
    all_to_all x1, blocking collectives, local(): lax.all_to_all(right_rows, 'gx', split_axis=0, concat_axis=2, tiled=True)  97.2 us
    all_to_all x1, blocking collectives, local(): lax.all_to_all(left_rows, 'gx', split_axis=0, concat_axis=2, tiled=True)  95.8 us
  transfers between devices with their start and end apart: 5, of which 4 were waited for; matrix products, arithmetic and copies ran while one was open for 7% of the time, Pallas kernels for 0%

commit v1 on v0

v1 whole, which is shorter than its diff:
```python
import functools
import itertools
import math

import jax
import jax.numpy as jnp
from jax import lax
from jax.experimental import pallas as pl
from jax.experimental.pallas import tpu as pltpu
from jax.sharding import PartitionSpec as P

epsilon = 1e-05
MESH = pl.DeviceIdType.MESH


def exchange_kernel(axes, sizes, take, put, x_ref, o_ref, send_sem, recv_sem, local_sem):
    me = tuple(lax.axis_index(axis) for axis in axes)
    offsets = [o for o in itertools.product(*(range(n) for n in sizes)) if any(o)]

    def peer_of(offset):
        return tuple(lax.rem(m + o, n) for m, o, n in zip(me, offset, sizes))

    barrier = pltpu.get_barrier_semaphore()
    for offset in offsets:
        pl.semaphore_signal(
            barrier, inc=1, device_id=dict(zip(axes, peer_of(offset))), device_id_type=MESH
        )
    pl.semaphore_wait(barrier, len(offsets))
    copies = []
    for index, offset in enumerate(offsets):
        peer = peer_of(offset)
        copy = pltpu.make_async_remote_copy(
            src_ref=take(x_ref, peer),
            dst_ref=put(o_ref, me),
            send_sem=send_sem.at[index],
            recv_sem=recv_sem.at[index],
            device_id=dict(zip(axes, peer)),
            device_id_type=MESH,
        )
        copy.start()
        copies.append(copy)
    own = pltpu.make_async_copy(take(x_ref, me), put(o_ref, me), local_sem)
    own.start()
    own.wait()
    for copy in copies:
        copy.wait()


def exchange(x, axes, shape, take, put, collective_id):
    sizes = tuple(lax.axis_size(axis) for axis in axes)
    count = math.prod(sizes) - 1
    moved = x.size * x.dtype.itemsize
    return pl.pallas_call(
        functools.partial(exchange_kernel, axes, sizes, take, put),
        out_shape=jax.ShapeDtypeStruct(shape, x.dtype),
        in_specs=[pl.BlockSpec(memory_space=pl.ANY)],
        out_specs=pl.BlockSpec(memory_space=pl.ANY),
        scratch_shapes=[
            pltpu.SemaphoreType.DMA((count,)),
            pltpu.SemaphoreType.DMA((count,)),
            pltpu.SemaphoreType.DMA,
        ],
        compiler_params=pltpu.CompilerParams(collective_id=collective_id, has_side_effects=True),
        cost_estimate=pl.CostEstimate(flops=0, bytes_accessed=20 * moved, transcendentals=0),
    )(x)


def normalize(values, gain):
    average = jnp.mean(values, axis=0, keepdims=True)
    centered = values - average
    spread = jnp.mean(jnp.square(centered), axis=0, keepdims=True)
    return (centered * lax.rsqrt(spread + epsilon) * gain).astype(jnp.bfloat16)


def project_kernel(x_ref, mask_ref, gain_ref, weight_ref, left_ref, right_ref, gate_ref):
    rows = x_ref.shape[0]
    h = left_ref.shape[1]
    gain = gain_ref[...]

    def body(row, carry):
        normed = normalize(x_ref[row].astype(jnp.float32), gain)
        mask = mask_ref[pl.ds(row, 1), :]

        def part(index):
            return jnp.dot(
                weight_ref[index * h : (index + 1) * h, :],
                normed,
                preferred_element_type=jnp.float32,
            )

        left_ref[row] = (mask * jax.nn.sigmoid(part(1)) * part(0)).astype(jnp.bfloat16)
        right_ref[row] = (mask * jax.nn.sigmoid(part(3)) * part(2)).astype(jnp.bfloat16)
        gate_ref[row] = jax.nn.sigmoid(part(4)).astype(jnp.bfloat16)
        return carry

    lax.fori_loop(0, rows, body, 0)


def finish_kernel(mix_ref, gate_ref, gain_ref, weight_ref, out_ref):
    gain = gain_ref[...]

    def body(row, carry):
        normed = normalize(mix_ref[row].astype(jnp.float32), gain)
        projected = jnp.dot(weight_ref[...], normed, preferred_element_type=jnp.float32)
        out_ref[row] = (gate_ref[row].astype(jnp.float32) * projected).astype(jnp.bfloat16)
        return carry

    lax.fori_loop(0, mix_ref.shape[0], body, 0)


def local(
    pair,
    pair_mask,
    in_gain,
    w_left,
    w_left_gate,
    w_right,
    w_right_gate,
    w_out_gate,
    out_gain,
    w_out,
):
    nx, nz = lax.axis_size("gx"), lax.axis_size("gz")
    channels, i_rows, k_columns = pair.shape
    c_all = channels * nz
    rows = i_rows // nz
    h_all = w_left.shape[1] * nz
    h_own = h_all // (nx * nz)
    stacked = jnp.stack([w_left, w_left_gate, w_right, w_right_gate, w_out_gate, w_out])
    weights = jnp.swapaxes(lax.all_gather(stacked, "gz", axis=2, tiled=True), 1, 2)
    gain_mix = lax.all_gather(out_gain, "gz", axis=0, tiled=True)
    mask_rows = lax.dynamic_slice_in_dim(
        pair_mask, lax.axis_index("gz") * rows, rows, axis=0
    ).astype(jnp.float32)

    gathered = exchange(
        jnp.swapaxes(pair, 0, 1),
        ("gz",),
        (rows, c_all, k_columns),
        lambda ref, dev: ref.at[pl.ds(dev[0] * rows, rows)],
        lambda ref, dev: ref.at[:, pl.ds(pl.multiple_of(dev[0] * channels, channels), channels)],
        0,
    )

    block = 8
    row_spec = pl.BlockSpec((block, c_all, k_columns), lambda i: (i, 0, 0))
    h_spec = pl.BlockSpec((block, h_all, k_columns), lambda i: (i, 0, 0))
    whole = lambda *shape: pl.BlockSpec(shape, lambda i: (0,) * len(shape))
    h_shape = jax.ShapeDtypeStruct((rows, h_all, k_columns), jnp.bfloat16)
    left_rows, right_rows, out_gate = pl.pallas_call(
        project_kernel,
        grid=(rows // block,),
        out_shape=(h_shape, h_shape, h_shape),
        in_specs=[
            row_spec,
            pl.BlockSpec((block, k_columns), lambda i: (i, 0)),
            whole(c_all, 1),
            whole(5 * h_all, c_all),
        ],
        out_specs=(h_spec, h_spec, h_spec),
    )(gathered, mask_rows, in_gain[:, None], weights[:5].reshape(5 * h_all, c_all))

    def block_of(ref, dev):
        return ref.at[
            :,
            pl.ds(pl.multiple_of(dev[1] * rows, rows), rows),
            pl.ds(pl.multiple_of(dev[0] * k_columns, k_columns), k_columns),
        ]

    def heads_of(ref, dev):
        return ref.at[pl.ds((dev[0] * nz + dev[1]) * h_own, h_own)]

    group_shape = (h_own, i_rows, k_columns * nx)
    right_group = exchange(
        jnp.swapaxes(right_rows, 0, 1), ("gx", "gz"), group_shape, heads_of, block_of, 1
    )
    right_all = lax.all_gather(right_group, "gy", axis=1, tiled=True)
    left_group = exchange(
        jnp.swapaxes(left_rows, 0, 1), ("gx", "gz"), group_shape, heads_of, block_of, 2
    )
    mixed = lax.dot_general(
        left_group,
        right_all,
        (((2,), (2,)), ((0,), (0,))),
        preferred_element_type=jnp.float32,
    ).astype(jnp.bfloat16)
    mix = exchange(
        mixed, ("gx", "gz"), (h_all, rows, k_columns), block_of, heads_of, 3
    )
    update = pl.pallas_call(
        finish_kernel,
        grid=(rows // block,),
        out_shape=h_shape,
        in_specs=[h_spec, h_spec, whole(h_all, 1), whole(h_all, h_all)],
        out_specs=h_spec,
    )(jnp.swapaxes(mix, 0, 1), out_gate, gain_mix[:, None], weights[5])
    result = exchange(
        update,
        ("gz",),
        (i_rows, channels, k_columns),
        lambda ref, dev: ref.at[:, pl.ds(pl.multiple_of(dev[0] * channels, channels), channels)],
        lambda ref, dev: ref.at[pl.ds(dev[0] * rows, rows)],
        4,
    )
    return jnp.swapaxes(result, 0, 1)


def solution(mesh):
    placed = (
        P("gz", "gy", "gx"),
        P("gy", "gx"),
        P(),
        P(None, "gz"),
        P(None, "gz"),
        P(None, "gz"),
        P(None, "gz"),
        P(None, "gz"),
        P("gz"),
        P(None, "gz"),
    )
    return jax.shard_map(
        local, mesh=mesh, in_specs=placed, out_specs=P("gz", "gy", "gx"), check_vma=False
    )
```

time: 1990 us -> 1110 us (0.56)
  waiting for transfers between devices: 1160 us -> 0.02 us
  Pallas kernels: 0 us -> 989 us
  blocking collectives: 384 us -> 23.7 us
  matrix products: 222 us -> 15.8 us
  other arithmetic: 82.3 us -> 1.57 us
  local copies, waits for them, and re-layouts: 115 us -> 68 us
    all_gather x3 -> x1, waiting for transfers between devices: 1080 us -> 0.01 us  [local(): right_all = lax.all_gather(right_group, 'gy', axis=1, tiled=True)]
    pallas_call x0 -> x7, Pallas kernels: none -> 989 us  [the longest x5 914 us: exchange(): pl.pallas_call(functools.partial(exchange_kernel, axes, sizes, take, put)...]
    all_to_all x3 -> x0, blocking collectives: 384 us -> none  [the longest x1 191 us: local(): lax.all_to_all(full_product, 'gx', split_axis=2, concat_axis=0, tiled=True)]
    dot_general x7 -> x1, matrix products: 222 us -> 15.8 us  [local(): lax.dot_general(left_group, right_all, (((2,), (2,)), ((0,), (0,))), pref...]
    psum x2 -> x0, waiting for transfers between devices: 77.9 us -> none  [the longest x1 39.3 us: local(): sum_terms = lax.psum(jnp.sum(mixed_sum, axis=0), 'gz')]
    all_to_all x5 -> x0, local copies, waits for them, and re-layouts: 63.4 us -> none  [the longest x2 21.6 us: local(): lax.all_to_all(right_rows, 'gx', split_axis=0, concat_axis=2, tiled=True)]
    reduce_sum x4 -> x0, other arithmetic: 44.7 us -> none  [the longest x1 12.2 us: local(): jnp.sum(jnp.square(mix_centered), axis=0)]
    pallas_call x0 -> x3, local copies, waits for them, and re-layouts: none -> 35.9 us  [the longest x2 24.3 us: local(): pl.pallas_call(project_kernel, grid=(rows // block,), out_shape=(h_shape,...]
  transfers between devices with their start and end apart: 5 -> 1, of which waited for: 4 -> 0; matrix products, arithmetic and copies ran while one was open for 7% -> 1% of each run, Pallas kernels for 0% -> 17%
where the time goes in v1:
time: 1110 us
  Pallas kernels  989 us (89%)
  local copies, waits for them, and re-layouts  68 us (6%)
  blocking collectives  23.7 us (2%)
  matrix products  15.8 us (1%)
  between operations  14 us (1%)
    pallas_call x5, Pallas kernels, exchange(): pl.pallas_call(functools.partial(exchange_kernel, axes, sizes, take, put)...  914 us
    pallas_call x1, Pallas kernels, local(): pl.pallas_call(project_kernel, grid=(rows // block,), out_shape=(h_shape,...  43.1 us
    pallas_call x1, Pallas kernels, local(): pl.pallas_call(finish_kernel, grid=(rows // block,), out_shape=h_shape, i...  31.5 us
    pallas_call x2, local copies, waits for them, and re-layouts, local(): pl.pallas_call(project_kernel, grid=(rows // block,), out_shape=(h_shape,...  24.3 us
  transfers between devices with their start and end apart: 1, of which 0 were waited for; matrix products, arithmetic and copies ran while one was open for 1% of the time, Pallas kernels for 17%

profile of v1, /device:TPU:8, one launch (start us, length us, event | category | flops | bytes accessed | tf_op | source)
XLA Modules:
  0.0 1112.1 jit_solution(16889234583801824666)
XLA Ops:
  6.5 0.0 all-gather.2.cloned.1.call-start
  6.5 0.7 constant_dynamic-update-slice_fusion.5
  7.2 1.4 copy.12.gain_ref
  8.6 0.7 constant_dynamic-update-slice_fusion.4
  9.3 0.7 constant_dynamic-update-slice_fusion.3
  10.0 0.7 constant_dynamic-update-slice_fusion.2
  10.7 0.7 constant_dynamic-update-slice_fusion.1
  11.4 0.7 constant_dynamic-update-slice_fusion
  12.1 14.2 %all_gather.9 = bf16[6,128,128]{1,2,0:T(8,128)(2,1)S(1)} all-gather(bf16[6,128,32]{1,2,0:T(8,128)(2,1)S(1)} %constant_dynamic-update-slice_fusion), channel_id=1, replica_groups=mesh['gx'=4,'gy'=2,'gz'=4] {'gz'}, dimensions={2}, use_global_device_ids=true | all-gather | bytes 245760 | tf_op jit(solution)/shard_map/all_gather | solution.py:130
  26.3 0.7 slice.8
  27.0 11.5 %copy.25 = bf16[32,512,256]{2,0,1:T(8,128)(2,1)} copy(bf16[32,512,256]{2,1,0:T(8,128)(2,1)} %param.10) | data formatting | bytes 16777216 | tf_op args[0]
  38.5 180.3 %shard_map.100.x_ref = bf16[128,128,256]{2,1,0:T(8,128)(2,1)} custom-call(bf16[512,32,256]{2,1,0:T(8,128)(2,1)} %bitcast.38), custom_call_target="tpu_custom_call" | custom-call | bytes 167772160 | tf_op jit(solution)/shard_map/pallas_call | solution.py:53
  218.9 1.6 dynamic-slice_convert_fusion.mask_ref
  220.4 43.1 %shard_map.101 = (bf16[128,128,256]{2,1,0:T(8,128)(2,1)}, bf16[128,128,256]{2,1,0:T(8,128)(2,1)}, bf16[128,128,256]{2,1,0:T(8,128)(2,1)}) custom-call(bf16[128,128,256]{2,1,0:T(8,128)(2,1)} %shard_map.100.x_ref, f32[128,256]{1,0:T(8,128)} %dynamic-slice_convert_fusion.mask_ref, f32[128,1]{1,0:T(8,128)} %copy.12.gain_ref, bf16[640,128]{1,0:T(8,128)(2,1)} %bitcast.41), custom_call_target="tpu_custom_call" | custom-call | tf_op jit(solution)/shard_map/pallas_call | solution.py:150
  263.5 11.4 %copy.23 = bf16[128,128,256]{2,0,1:T(8,128)(2,1)} copy(bf16[128,128,256]{2,1,0:T(8,128)(2,1)} %get-tuple-element.9) | data formatting | bytes 16777216 | tf_op jit(solution)/shard_map/pallas_call | solution.py:150
  274.9 184.0 %shard_map.103 = bf16[8,512,1024]{2,1,0:T(8,128)(2,1)} custom-call(bf16[128,128,256]{2,1,0:T(8,128)(2,1)} %bitcast.35), custom_call_target="tpu_custom_call" | custom-call | bytes 167772160 | tf_op jit(solution)/shard_map/pallas_call | solution.py:53
  458.9 0.0 copy-start.1
  458.9 0.0 copy-start
  459.0 0.0 all-gather.2.cloned.1.call-update
  459.0 0.6 copy-done.1
  459.6 0.6 dynamic-slice
  460.7 0.0 copy-done
  460.7 0.2 dynamic-update-slice
  461.0 9.5 all-reduce
  470.5 0.7 copy.16.gain_ref
  471.3 12.9 %copy.24 = bf16[128,128,256]{2,0,1:T(8,128)(2,1)} copy(bf16[128,128,256]{2,1,0:T(8,128)(2,1)} %get-tuple-element.8) | data formatting | bytes 16777216 | tf_op jit(solution)/shard_map/pallas_call | solution.py:150
  484.2 184.1 %shard_map.102 = bf16[8,512,1024]{2,1,0:T(8,128)(2,1)} custom-call(bf16[128,128,256]{2,1,0:T(8,128)(2,1)} %bitcast.36), custom_call_target="tpu_custom_call" | custom-call | bytes 167772160 | tf_op jit(solution)/shard_map/pallas_call | solution.py:53
  668.3 0.6 slice_bitcast_fusion.weight_ref
  668.9 0.0 all-gather.2.cloned.1.call-done
  668.9 15.8 %convolution_convert_fusion.x_ref = bf16[8,512,1024]{2,1,0:T(8,128)(2,1)} fusion(bf16[8,512,1024]{2,1,0:T(8,128)(2,1)} %shard_map.102, bf16[8,1024,1024]{2,1,0:T(8,128)(2,1)} %all-gather.2.cloned.1.call-done), kind=kOutput, calls=%fused_computation.4 | convolution fusion | flops 8594128896 | bytes 33554432 | tf_op jit(solution)/shard_map/dot_general | solution.py:181
  684.7 184.1 %shard_map.104 = bf16[128,128,256]{2,1,0:T(8,128)(2,1)} custom-call(bf16[8,512,1024]{2,1,0:T(8,128)(2,1)} %convolution_convert_fusion.x_ref), custom_call_target="tpu_custom_call" | custom-call | bytes 167772160 | tf_op jit(solution)/shard_map/pallas_call | solution.py:53
  868.8 11.5 %copy.22 = bf16[128,128,256]{2,0,1:T(8,128)(2,1)} copy(bf16[128,128,256]{2,1,0:T(8,128)(2,1)} %shard_map.104) | data formatting | bytes 16777216 | tf_op jit(solution)/shard_map/pallas_call | solution.py:53
  880.3 31.5 %shard_map.105.x_ref = bf16[128,128,256]{2,1,0:T(8,128)(2,1)} custom-call(bf16[128,128,256]{2,1,0:T(8,128)(2,1)} %bitcast.34, bf16[128,128,256]{2,1,0:T(8,128)(2,1)} %get-tuple-element.10.gate_ref, f32[128,1]{1,0:T(8,128)} %copy.16.gain_ref, bf16[128,128]{1,0:T(8,128)(2,1)} %slice_bitcast_fusion.weight_ref), custom_call_target="tpu_custom_call" | custom-call | tf_op jit(solution)/shard_map/pallas_call | solution.py:190
  911.8 181.9 %shard_map.106 = bf16[512,32,256]{2,1,0:T(8,128)(2,1)} custom-call(bf16[128,128,256]{2,1,0:T(8,128)(2,1)} %shard_map.105.x_ref), custom_call_target="tpu_custom_call" | custom-call | bytes 167772160 | tf_op jit(solution)/shard_map/pallas_call | solution.py:53
  1093.8 11.5 %copy.17 = bf16[32,512,256]{2,1,0:T(8,128)(2,1)} copy(bf16[32,512,256]{2,0,1:T(8,128)(2,1)} %bitcast.37) | data formatting | bytes 16777216 | tf_op jit(solution)/shard_map/transpose | solution.py:205
  (1 shorter events, 0.0 us)
Async XLA Ops:
  6.5 662.3 %all-gather.2.cloned.1.call-start = ((), (), s32[]{:S(2)}) async-start(), calls=%async_computation | async-start | bytes 25165824 | tf_op jit(solution)/shard_map/all_gather | solution.py:177
  458.9 0.7 copy-start.1
  458.9 1.8 copy-start
Sparse Core Ops, SparseCore 0:
  459.1 30.4 all-gather.1
